TPU v7x, 32 devices: a whole 2x2x4 slice. The times are simulated.
32 devices in a mesh: tok: 8 (over z, y), unit: 4 (over x, core).
Axes of the slice: x: 2, y: 2, z: 4, core: 2. Of those that a mesh axis runs over, the one named last changes fastest.
Arguments:
- act_a: bfloat16 [16384, 3072], P('tok', 'unit'), may hold values from -4000 to 4000
- act_b: bfloat16 [16384, 3072], P(('tok', 'unit')), may hold values from -4000 to 4000
Outputs:
- correlation: float32 [3072, 3072], P('tok', 'unit')
All inputs are finite; a program needn't handle non-finite values.
Results may differ from a plain program's by a relative error of at most 0.0003.
Values may be sent and summed in bfloat16 or wider, within the bound.
A program may use at most 128 MiB of HBM per device.

v0:
```python
import functools

import jax
import jax.numpy as jnp
from jax import lax
from jax.experimental import pallas as pl
from jax.experimental.pallas import tpu as pltpu
from jax.sharding import PartitionSpec as P

MESH = pl.DeviceIdType.MESH
LANES = 128
SPAN = 240.0
BASE = 120.0


def contract_tokens(left, right):
    return lax.dot_general(
        left, right, (((0,), (0,)), ((), ())), preferred_element_type=jnp.float32
    )


def plain(act_a, act_b):
    token_rows = act_a.shape[0]
    units = act_b.shape[1]
    groups = lax.axis_size("tok")
    band = units // groups
    total_tokens = token_rows * groups
    wide_a = act_a.astype(jnp.float32)
    first_total = jnp.sum(wide_a, axis=0)
    first_square = jnp.sum(wide_a * wide_a, axis=0)
    piece = lax.all_gather(act_b, "unit", axis=0, tiled=True)
    product = contract_tokens(piece, act_a)
    wide_piece = piece.astype(jnp.float32)
    second_total = jnp.sum(wide_piece, axis=0)
    second_square = jnp.sum(wide_piece * wide_piece, axis=0)
    shares = lax.psum_scatter(product, "tok", scatter_dimension=0, tiled=True)
    first_all, first_square_all, second_all, second_square_all = lax.psum(
        (first_total, first_square, second_total, second_square), "tok"
    )
    offset = lax.axis_index("tok") * band
    second_own = lax.dynamic_slice_in_dim(second_all, offset, band, 0)
    second_square_own = lax.dynamic_slice_in_dim(second_square_all, offset, band, 0)
    mean_a = first_all / total_tokens
    var_a = first_square_all / total_tokens - mean_a * mean_a
    mean_b = second_own / total_tokens
    var_b = second_square_own / total_tokens - mean_b * mean_b
    centered = shares / total_tokens - mean_b[:, None] * mean_a[None, :]
    return centered / (jnp.sqrt(var_b + 1e-05)[:, None] * jnp.sqrt(var_a + 1e-05)[None, :])


def schedule(rings, parts):
    crosses, keeps = rings * parts, (rings - 1) * parts
    events = sorted(
        [((k + 0.25) / crosses, 0, k) for k in range(crosses)]
        + [((k + 1) / keeps, 1, k) for k in range(keeps)]
    )
    slots = [(kind, k) for _, kind, k in events] + [(1, keeps + i) for i in range(parts)]
    place = {slot: s for s, slot in enumerate(slots)}
    orders = []
    for r in range(rings):
        behind = lambda d: r if d > r else rings - 1 - r
        others = [d for d in range(rings) if d != r]
        orders.append(sorted(others, key=lambda d: (-abs(d - r), -behind(d), d)) + [r])
    done = [{} for _ in range(rings)]
    merges = [[0] * len(slots) for _ in range(rings)]
    for s in range(crosses + keeps):
        for r in range(rings):
            k = len(done[r])
            if k == keeps or place[1, k] > s or place[0, k] + 3 > s:
                continue
            d, i = orders[r][k // parts], k % parts
            before = r - 1 if d > r else r + 1
            if 0 <= before < rings and done[before].get((d, i), s) + 3 > s:
                continue
            done[r][d, i] = s
            merges[r][s] = k + 1
    complete = all(len(d) == keeps for d in done)
    return slots, orders, merges, complete


def pick(values, i):
    out = values[-1]
    for k in reversed(range(len(values) - 1)):
        if values[k] != values[k + 1] or not isinstance(out, (int, float)):
            out = jnp.where(i == k, values[k], out)
    return out


def pick_row(rows, r, i):
    out = None
    unique = []
    for row in rows:
        if row not in unique:
            unique.append(row)
    for row in unique:
        mine = pick(row, i)
        if out is None:
            out = mine
        else:
            here = functools.reduce(jnp.logical_or, [r == k for k in range(len(rows)) if rows[k] == row])
            out = jnp.where(here, mine, out)
    return out


def column(row):
    return jnp.transpose(jnp.broadcast_to(row, (LANES, LANES)))


def spread(square, total, share):
    return jnp.maximum(square - total * total * share, square * 1e-5 + 1e-30)


def encode(q):
    size = jnp.exp2(jnp.minimum(jnp.abs(q), 1.04) * SPAN - BASE)
    return jnp.where(q < 0, -size, size).astype(jnp.bfloat16)


def decode(code):
    y = code.astype(jnp.float32)
    size = jnp.log2(jnp.abs(y)) + BASE
    return jnp.where(y < 0, -size, size)


def kernel(groups, plan, a_hbm, b_hbm, out, a, g, held, cross_out, cross_in, far_out, far_in,
           sa_own, sa_near, sa_pair, sa_in, sa_run, sa_stat, sb_half, sb_mine, sb_near, sb_run, sb_in,
           a_sem, b_sem, px_send, px_recv, nx_send, nx_recv, fw_send, fw_recv,
           c_send, c_recv, cb_send, cb_recv, f_send, f_recv, fb_send, fb_recv,
           ca_send, ca_recv, fa_send, fa_recv):
    slots, orders, merges, _ = plan
    t = lax.axis_index("tok")
    u = lax.axis_index("unit")
    rows, units = b_hbm.shape
    tokens, own = a.shape
    band = units // groups
    parts = band // LANES
    rings = groups // 2
    crosses = rings * parts
    keeps = crosses - parts
    steps = len(slots)
    half = tokens // 2
    r = t // 2
    y = t % 2
    side = u // 2
    partner = u + 1 - 2 * (u % 2)
    across = (u + 2) % 4
    near = t + 1 - 2 * y
    shares = [1.0 / (2 * tokens * max(k, 1)) for k in range(rings + 1)]
    packed = [kind + 2 * (k // parts) + 2048 * (k % parts) for kind, k in slots]

    def slot(s):
        code = pick(packed, s)
        kind, p, i = code % 2, (code // 2) % 1024, code // 2048
        return kind, p, i

    def bound(p):
        return pick_row(orders, r, p)

    def columns(kind, p, i):
        owner = bound(p) * 2 + jnp.where(kind == 0, 1 - y, y)
        return pl.ds(pl.multiple_of(owner * band + i * LANES, LANES), LANES)

    def block(ref, who, cols):
        return ref.at[pl.ds(pl.multiple_of(who * rows, rows), rows), cols]

    def remote(src, dst, send, recv, tt, uu):
        return pltpu.make_async_remote_copy(
            src_ref=src, dst_ref=dst, send_sem=send, recv_sem=recv,
            device_id=(tt, uu), device_id_type=MESH)

    def to_partner(s, cols):
        return remote(b_hbm.at[:, cols], block(g, u, cols), px_send.at[0], px_recv.at[s], t, partner)

    def to_across(s, cols):
        return remote(b_hbm.at[:, cols], block(g, u, cols), nx_send.at[0], nx_recv.at[s], t, across)

    def forward(s, cols):
        return remote(block(g, across, cols), block(g, across, cols), fw_send.at[0], fw_recv.at[s],
                      t, partner)

    def send_cross(k):
        return remote(cross_out.at[k], cross_in.at[k], c_send.at[0], c_recv.at[k], near, u)

    def send_cross_sums(k):
        return remote(sb_mine.at[k], sb_near.at[k], cb_send.at[0], cb_recv.at[k], near, u)

    def send_far(k, j, tt):
        return remote(far_out.at[k], far_in.at[j], f_send.at[0], f_recv.at[j], tt, u)

    def send_far_sums(k, j, tt):
        return remote(sb_run.at[k], sb_in.at[j], fb_send.at[0], fb_recv.at[j], tt, u)

    send_near_a = remote(sa_own, sa_near, ca_send.at[0], ca_recv.at[0], near, u)

    def send_run_a(way):
        tt = t + 2 if way == 0 else t - 2
        return remote(sa_run.at[way], sa_in.at[way], fa_send.at[way], fa_recv.at[way], tt, u)

    a_copy = pltpu.make_async_copy(a_hbm, a, a_sem)
    own_rows = pl.ds(pl.multiple_of(u * rows, rows), rows)
    b_copy = pltpu.make_async_copy(b_hbm, g.at[own_rows, :], b_sem)

    barrier = pltpu.get_barrier_semaphore()

    def greet(tt, uu):
        pl.semaphore_signal(barrier, inc=1, device_id=(tt, uu), device_id_type=MESH)

    greet(t, across)
    greet(t, partner)
    greet(near, u)

    @pl.when(r > 0)
    def _():
        greet(t - 2, u)

    @pl.when(r < rings - 1)
    def _():
        greet(t + 2, u)

    a_copy.start()
    b_copy.start()
    pl.semaphore_wait(barrier, 3 + jnp.where(r > 0, 1, 0) + jnp.where(r < rings - 1, 1, 0))

    @pl.loop(0, steps)
    def _(s):
        cols = columns(*slot(s))
        to_across(s, cols).start()
        to_partner(s, cols).start()

    a_copy.wait()
    b_copy.wait()
    chunk = 128

    def sum_rows(wide):
        wide = wide.astype(jnp.float32).reshape(wide.shape[0] // 8, 8, wide.shape[1])
        return jnp.sum(wide, axis=0), jnp.sum(wide * wide, axis=0)

    def body(i, carry):
        total, square = sum_rows(a[pl.ds(pl.multiple_of(i * chunk, chunk), chunk), :])
        return carry[0] + total, carry[1] + square

    zero = jnp.zeros((8, own), jnp.float32)
    total, square = lax.fori_loop(0, tokens // chunk, body, (zero, zero))
    sa_own[...] = jnp.zeros((8, own), jnp.float32)
    sa_own[0:1, :] = jnp.sum(total, axis=0, keepdims=True)
    sa_own[1:2, :] = jnp.sum(square, axis=0, keepdims=True)
    send_near_a.start()

    def tiles():
        return [slice(c * LANES, (c + 1) * LANES) for c in range(own // LANES)]

    def early(hold, cols):
        mine = pl.ds(pl.multiple_of(side * half, half), half)
        lhs = g[mine, cols]
        held[hold] = contract_tokens(lhs, a[mine, :])
        total, square = sum_rows(lhs)
        sb_half[0] = total
        sb_half[1] = square

    def late(hold, slot_sums, cols):
        theirs = pl.ds(pl.multiple_of((1 - side) * half, half), half)
        lhs = g[theirs, cols]
        held[hold] = held[hold] + contract_tokens(lhs, a[theirs, :])
        total, square = sum_rows(lhs)
        sb_mine[slot_sums] = jnp.zeros((8, LANES), jnp.float32)
        sb_mine[slot_sums, 0:1, :] = jnp.sum(sb_half[0] + total, axis=0, keepdims=True)
        sb_mine[slot_sums, 1:2, :] = jnp.sum(sb_half[1] + square, axis=0, keepdims=True)

    def put(target, k, hold, sb, sa, share):
        tb, qb = sb[0:1, :], sb[1:2, :]
        tb_col = column(tb * share)
        scale_col = column(lax.rsqrt(spread(qb, tb, share)))
        for cols in tiles():
            ta = sa[0:1, cols]
            scale = lax.rsqrt(spread(sa[1:2, cols], ta, share))
            q = (held[hold, :, cols] - tb_col * ta) * (scale_col * scale)
            target[k, :, cols] = encode(q)

    def take(hold, source, k, sb, sa, share):
        tb, qb = sb[0:1, :], sb[1:2, :]
        tb_col = column(tb * share)
        norm_col = column(jnp.sqrt(spread(qb, tb, share)) * (1.0 / SPAN))
        for cols in tiles():
            ta = sa[0:1, cols]
            norm = jnp.sqrt(spread(sa[1:2, cols], ta, share))
            held[hold, :, cols] = held[hold, :, cols] + (
                decode(source[k, :, cols]) * (norm_col * norm) + tb_col * ta)

    def take_near(k):
        send_cross_sums(k).wait_recv()
        send_cross(k).wait_recv()
        take(k, cross_in, k, sb_near.at[k], sa_near, 1.0 / tokens)

    def take_far(way, k, j):
        tt = t + 2 - 4 * way
        send_far_sums(0, j, tt).wait_recv()
        send_far(0, j, tt).wait_recv()
        count = jnp.where(way == 0, r, rings - 1 - r)
        take(k, far_in, j, sb_in.at[j], sa_in.at[way], pick(shares, count))

    def merge(k):
        p, i = k // parts, k % parts
        d = bound(p)
        way = jnp.where(d > r, 0, 1)
        j = (way * rings + d) * parts + i
        take_near(k)
        sb_run[k] = sb_mine[crosses + k] + sb_near[k]
        count = jnp.where(way == 0, r, rings - 1 - r)

        @pl.when(count > 0)
        def _():
            take_far(way, k, j)
            sb_run[k] = sb_run[k] + sb_in[j]

        put(far_out, k, k, sb_run.at[k], sa_run.at[way], pick(shares, count + 1))
        tt = t + 2 - 4 * way
        send_far(k, j, tt).start()
        send_far_sums(k, j, tt).start()

    def exchange_a(s):
        @pl.when(s == 1)
        def _():
            send_near_a.wait_recv()
            sa_pair[...] = sa_own[...] + sa_near[...]

        for way, ready in ((0, r + 1), (1, rings - r)):
            first = (r == 0) if way == 0 else (r == rings - 1)
            final = (r == rings - 1) if way == 0 else (r == 0)

            @pl.when(jnp.logical_and(s == ready, first))
            def _():
                sa_in[way] = jnp.zeros((8, own), jnp.float32)
                sa_run[way] = sa_pair[...]

            @pl.when(jnp.logical_and(s == ready, jnp.logical_not(first)))
            def _():
                send_run_a(way).wait_recv()
                sa_run[way] = sa_pair[...] + sa_in[way]

            @pl.when(jnp.logical_and(s == ready, jnp.logical_not(final)))
            def _():
                send_run_a(way).start()

    @pl.loop(0, steps - parts)
    def _(s):
        kind, p, i = slot(s)
        cols = columns(kind, p, i)
        k = p * parts + i
        hold = jnp.where(kind == 0, crosses, k)
        to_partner(s, cols).wait_recv()
        early(hold, cols)
        to_across(s, cols).wait_recv()
        forward(s, cols).start()
        exchange_a(s)
        forward(s, cols).wait_recv()
        late(hold, kind * crosses + k, cols)

        @pl.when(kind == 0)
        def _():
            put(cross_out, k, hold, sb_mine.at[k], sa_own, 1.0 / tokens)
            send_cross(k).start()
            send_cross_sums(k).start()

        pair = pick_row(merges, r, s)

        @pl.when(pair > 0)
        def _():
            merge(pair - 1)

    whole_a = sa_pair[...] + sa_in[0] + sa_in[1]
    total_tokens = tokens * groups
    mean_a = whole_a[0:1, :] * (1.0 / total_tokens)
    var_a = whole_a[1:2, :] * (1.0 / total_tokens) - mean_a * mean_a
    sa_stat[0:1, :] = mean_a
    sa_stat[1:2, :] = 1.0 / jnp.sqrt(var_a + 1e-05)

    @pl.loop(0, parts)
    def _(i):
        s = steps - parts + i
        k = keeps + i
        cols = pl.ds(pl.multiple_of(t * band + i * LANES, LANES), LANES)
        to_partner(s, cols).wait_recv()
        early(k, cols)
        to_across(s, cols).wait_recv()
        forward(s, cols).start()
        take_near(k)
        sb_half[2] = sb_near[k]
        for way, some in ((0, r > 0), (1, r < rings - 1)):
            @pl.when(some)
            def _():
                j = (way * rings + r) * parts + i
                take_far(way, k, j)
                sb_half[2] = sb_half[2] + sb_in[j]

        forward(s, cols).wait_recv()
        late(k, crosses + k, cols)
        whole_b = sb_half[2] + sb_mine[crosses + k]
        mean_b = whole_b[0:1, :] * (1.0 / total_tokens)
        var_b = whole_b[1:2, :] * (1.0 / total_tokens) - mean_b * mean_b
        mean_col = column(mean_b)
        inv_col = column(1.0 / jnp.sqrt(var_b + 1e-05))
        lanes = pl.ds(pl.multiple_of(i * LANES, LANES), LANES)
        for c in tiles():
            centered = held[k, :, c] * (1.0 / total_tokens) - mean_col * sa_stat[0:1, c]
            out[lanes, c] = centered * (inv_col * sa_stat[1:2, c])

    send_near_a.wait_send()

    @pl.when(r < rings - 1)
    def _():
        send_run_a(0).wait_send()

    @pl.when(r > 0)
    def _():
        send_run_a(1).wait_send()

    own_b = g.at[own_rows, :]
    remote(b_hbm, own_b, nx_send.at[0], nx_recv.at[0], t, across).wait_send()
    remote(b_hbm, own_b, px_send.at[0], px_recv.at[0], t, partner).wait_send()
    remote(own_b, own_b, fw_send.at[0], fw_recv.at[0], t, partner).wait_send()
    remote(cross_out, cross_in, c_send.at[0], c_recv.at[0], near, u).wait_send()
    remote(sb_near, sb_near, cb_send.at[0], cb_recv.at[0], near, u).wait_send()
    remote(far_out, far_out, f_send.at[0], f_recv.at[0], near, u).wait_send()
    remote(sb_run, sb_run, fb_send.at[0], fb_recv.at[0], near, u).wait_send()


def fused(groups, plan, act_a, act_b):
    tokens, own = act_a.shape
    rows, units = act_b.shape
    band = units // groups
    parts = band // LANES
    rings = groups // 2
    crosses = rings * parts
    keeps = crosses - parts
    steps = 2 * crosses
    dma = lambda n: pltpu.SemaphoreType.DMA((n,))
    bf16 = lambda *shape: pltpu.VMEM(shape, jnp.bfloat16)
    f32 = lambda *shape: pltpu.VMEM(shape, jnp.float32)
    return pl.pallas_call(
        functools.partial(kernel, groups, plan),
        out_shape=jax.ShapeDtypeStruct((band, own), jnp.float32),
        in_specs=[pl.BlockSpec(memory_space=pltpu.HBM)] * 2,
        out_specs=pl.BlockSpec(memory_space=pltpu.VMEM),
        scratch_shapes=[
            bf16(tokens, own),
            bf16(tokens, units),
            f32(crosses + 1, LANES, own),
            bf16(crosses, LANES, own),
            bf16(crosses, LANES, own),
            bf16(keeps, LANES, own),
            bf16(2 * crosses, LANES, own),
            f32(8, own), f32(8, own), f32(8, own),
            f32(2, 8, own), f32(2, 8, own), f32(8, own),
            f32(3, 8, LANES),
            f32(2 * crosses, 8, LANES), f32(crosses, 8, LANES),
            f32(keeps, 8, LANES), f32(2 * crosses, 8, LANES),
            pltpu.SemaphoreType.DMA, pltpu.SemaphoreType.DMA,
            dma(1), dma(steps),
            dma(1), dma(steps),
            dma(1), dma(steps),
            dma(1), dma(crosses),
            dma(1), dma(crosses),
            dma(1), dma(2 * crosses),
            dma(1), dma(2 * crosses),
            dma(1), dma(1),
            dma(2), dma(2),
        ],
        compiler_params=pltpu.CompilerParams(
            collective_id=0, has_side_effects=True, vmem_limit_bytes=52000 * 1024
        ),
        name="gather_correlate",
    )(act_a, act_b)


def solution(mesh):
    groups, split = mesh.shape["tok"], mesh.shape["unit"]

    def per_device(act_a, act_b):
        band = act_b.shape[1] // groups
        whole = act_a.shape[0] % 256 == 0 and act_a.shape[1] % LANES == 0
        if split == 4 and groups % 2 == 0 and groups > 4 and band % LANES == 0 and whole:
            plan = schedule(groups // 2, band // LANES)
            if plan[-1]:
                return fused(groups, plan, act_a, act_b)
        return plain(act_a, act_b)

    placed = (P("tok", "unit"), P(("tok", "unit"), None))
    return jax.shard_map(
        per_device, mesh=mesh, in_specs=placed, out_specs=P("tok", "unit"), check_vma=False
    )
```

profile of v0, /device:TPU:0, one launch (start us, length us, event | category | flops | bytes accessed | tf_op | source)
XLA Modules:
  0.0 76.9 jit_solution(3845265188984279208)
XLA Ops:
  0.0 75.9 %gather_correlate.1 = f32[384,768]{1,0:T(8,128)S(1)} custom-call(bf16[2048,768]{1,0:T(8,128)(2,1)} %a_hbm.1, bf16[512,3072]{1,0:T(8,128)(2,1)} %b_hbm.1), custom_call_target="tpu_custom_call" | custom-call | tf_op jit(solution)/shard_map/gather_correlate/pallas_call | solution.py:438
  75.9 1.0 %copy.4 = f32[384,768]{1,0:T(8,128)} copy(f32[384,768]{1,0:T(8,128)S(1)} %gather_correlate.1) | data formatting | bytes 2359296
where the time goes:
time: 77.1 us; the launch traced here: 76.9 us
  Pallas kernels  75.9 us (98%)
  local copies, waits for them, and re-layouts  1.02 us (1%)
    pallas_call x1, Pallas kernels, fused(): pl.pallas_call(functools.partial(kernel, groups, plan), out_shape=jax.Sha...  75.9 us

commit v1 on v0

--- a/solution.py
+++ b/solution.py
@@ -11,6 +11,8 @@
 LANES = 128
 SPAN = 240.0
 BASE = 120.0
+AHEAD = 4
+BUNCHES = 4
 
 
 def contract_tokens(left, right):
@@ -124,7 +126,7 @@
 def kernel(groups, plan, a_hbm, b_hbm, out, a, g, held, cross_out, cross_in, far_out, far_in,
            sa_own, sa_near, sa_pair, sa_in, sa_run, sa_stat, sb_half, sb_mine, sb_near, sb_run, sb_in,
            a_sem, b_sem, px_send, px_recv, nx_send, nx_recv, fw_send, fw_recv,
-           c_send, c_recv, cb_send, cb_recv, f_send, f_recv, fb_send, fb_recv,
+           c_send, cb_send, c_recv, f_send, fb_send, f_recv,
            ca_send, ca_recv, fa_send, fa_recv):
     slots, orders, merges, _ = plan
     t = lax.axis_index("tok")
@@ -137,6 +139,8 @@
     crosses = rings * parts
     keeps = crosses - parts
     steps = len(slots)
+    main = steps - parts
+    bunch = steps // BUNCHES
     half = tokens // 2
     r = t // 2
     y = t % 2
@@ -168,26 +172,55 @@
             device_id=(tt, uu), device_id_type=MESH)
 
     def to_partner(s, cols):
-        return remote(b_hbm.at[:, cols], block(g, u, cols), px_send.at[0], px_recv.at[s], t, partner)
+        return remote(b_hbm.at[:, cols], block(g, u, cols), px_send.at[0], px_recv.at[s // bunch], t, partner)
 
     def to_across(s, cols):
-        return remote(b_hbm.at[:, cols], block(g, u, cols), nx_send.at[0], nx_recv.at[s], t, across)
+        return remote(b_hbm.at[:, cols], block(g, u, cols), nx_send.at[0], nx_recv.at[s % (2 * AHEAD)],
+                      t, across)
 
     def forward(s, cols):
-        return remote(block(g, across, cols), block(g, across, cols), fw_send.at[0], fw_recv.at[s],
-                      t, partner)
+        return remote(block(g, across, cols), block(g, across, cols), fw_send.at[0],
+                      fw_recv.at[2 * (s % 2)], t, partner)
+
+    def piece(who, h, cols):
+        size = rows // 2
+        return g.at[pl.ds(pl.multiple_of(who * rows + h * size, size), size), cols]
+
+    def last_across(i, h, cols):
+        return remote(b_hbm.at[pl.ds(h * (rows // 2), rows // 2), cols], piece(u, h, cols),
+                      nx_send.at[0], nx_recv.at[2 * AHEAD + 2 * i + h], t, across)
+
+    def last_forward(s, h, cols):
+        return remote(piece(across, h, cols), piece(across, h, cols), fw_send.at[0],
+                      fw_recv.at[2 * (s % 2) + h], t, partner)
+
+    def issue_across(s):
+        cols = columns(*slot(s))
+
+        @pl.when(s < main)
+        def _():
+            to_across(s, cols).start()
+
+        @pl.when(jnp.logical_and(s >= main, s < steps))
+        def _():
+            for h in (0, 1):
+                last_across(s - main, h, cols).start()
 
     def send_cross(k):
         return remote(cross_out.at[k], cross_in.at[k], c_send.at[0], c_recv.at[k], near, u)
 
     def send_cross_sums(k):
-        return remote(sb_mine.at[k], sb_near.at[k], cb_send.at[0], cb_recv.at[k], near, u)
+        return remote(sb_mine.at[k], sb_near.at[k], cb_send.at[0], c_recv.at[k], near, u)
+
+    def both(sem):
+        some = g.at[pl.ds(0, own + 16), pl.ds(0, LANES)]
+        return pltpu.make_async_copy(some, some, sem)
 
     def send_far(k, j, tt):
         return remote(far_out.at[k], far_in.at[j], f_send.at[0], f_recv.at[j], tt, u)
 
     def send_far_sums(k, j, tt):
-        return remote(sb_run.at[k], sb_in.at[j], fb_send.at[0], fb_recv.at[j], tt, u)
+        return remote(sb_run.at[k], sb_in.at[j], fb_send.at[0], f_recv.at[j], tt, u)
 
     send_near_a = remote(sa_own, sa_near, ca_send.at[0], ca_recv.at[0], near, u)
 
@@ -222,9 +255,11 @@
 
     @pl.loop(0, steps)
     def _(s):
-        cols = columns(*slot(s))
-        to_across(s, cols).start()
-        to_partner(s, cols).start()
+        @pl.when(s < AHEAD)
+        def _():
+            issue_across(s)
+
+        to_partner(s, columns(*slot(s))).start()
 
     a_copy.wait()
     b_copy.wait()
@@ -256,14 +291,27 @@
         sb_half[0] = total
         sb_half[1] = square
 
-    def late(hold, slot_sums, cols):
+    def part(hold, start, size, cols):
+        some = pl.ds(pl.multiple_of(start, size), size)
+        lhs = g[some, cols]
+        held[hold] = held[hold] + contract_tokens(lhs, a[some, :])
+        total, square = sum_rows(lhs)
+        sb_half[0] = sb_half[0] + total
+        sb_half[1] = sb_half[1] + square
+
+    def finish_sums(k):
+        sb_mine[k] = jnp.zeros((8, LANES), jnp.float32)
+        sb_mine[k, 0:1, :] = jnp.sum(sb_half[0], axis=0, keepdims=True)
+        sb_mine[k, 1:2, :] = jnp.sum(sb_half[1], axis=0, keepdims=True)
+
+    def late(hold, k, cols):
         theirs = pl.ds(pl.multiple_of((1 - side) * half, half), half)
         lhs = g[theirs, cols]
         held[hold] = held[hold] + contract_tokens(lhs, a[theirs, :])
         total, square = sum_rows(lhs)
-        sb_mine[slot_sums] = jnp.zeros((8, LANES), jnp.float32)
-        sb_mine[slot_sums, 0:1, :] = jnp.sum(sb_half[0] + total, axis=0, keepdims=True)
-        sb_mine[slot_sums, 1:2, :] = jnp.sum(sb_half[1] + square, axis=0, keepdims=True)
+        sb_half[0] = sb_half[0] + total
+        sb_half[1] = sb_half[1] + square
+        finish_sums(k)
 
     def put(target, k, hold, sb, sa, share):
         tb, qb = sb[0:1, :], sb[1:2, :]
@@ -286,35 +334,42 @@
                 decode(source[k, :, cols]) * (norm_col * norm) + tb_col * ta)
 
     def take_near(k):
-        send_cross_sums(k).wait_recv()
-        send_cross(k).wait_recv()
+        both(c_recv.at[k]).wait()
         take(k, cross_in, k, sb_near.at[k], sa_near, 1.0 / tokens)
 
     def take_far(way, k, j):
-        tt = t + 2 - 4 * way
-        send_far_sums(0, j, tt).wait_recv()
-        send_far(0, j, tt).wait_recv()
+        both(f_recv.at[j]).wait()
         count = jnp.where(way == 0, r, rings - 1 - r)
         take(k, far_in, j, sb_in.at[j], sa_in.at[way], pick(shares, count))
 
-    def merge(k):
+    def route(k):
         p, i = k // parts, k % parts
         d = bound(p)
         way = jnp.where(d > r, 0, 1)
-        j = (way * rings + d) * parts + i
+        count = jnp.where(way == 0, r, rings - 1 - r)
+        distance = jnp.where(way == 0, d - r, r - d)
+        return way, count, (way * (rings - 1) + distance) * parts + i
+
+    def collect(k):
+        way, count, j = route(k)
         take_near(k)
+
+        @pl.when(count > 0)
+        def _():
+            take_far(way, k, j)
+
+    def pass_on(k):
+        way, count, j = route(k)
         sb_run[k] = sb_mine[crosses + k] + sb_near[k]
-        count = jnp.where(way == 0, r, rings - 1 - r)
 
         @pl.when(count > 0)
         def _():
-            take_far(way, k, j)
             sb_run[k] = sb_run[k] + sb_in[j]
 
         put(far_out, k, k, sb_run.at[k], sa_run.at[way], pick(shares, count + 1))
         tt = t + 2 - 4 * way
-        send_far(k, j, tt).start()
-        send_far_sums(k, j, tt).start()
+        send_far(k, j - parts, tt).start()
+        send_far_sums(k, j - parts, tt).start()
 
     def exchange_a(s):
         @pl.when(s == 1)
@@ -340,17 +395,29 @@
             def _():
                 send_run_a(way).start()
 
-    @pl.loop(0, steps - parts)
+    def partner_ready(s):
+        @pl.when(s % bunch == 0)
+        def _():
+            to_partner(s, pl.ds(0, LANES * bunch)).wait_recv()
+
+    @pl.loop(0, main)
     def _(s):
         kind, p, i = slot(s)
         cols = columns(kind, p, i)
         k = p * parts + i
         hold = jnp.where(kind == 0, crosses, k)
-        to_partner(s, cols).wait_recv()
+        partner_ready(s)
         early(hold, cols)
         to_across(s, cols).wait_recv()
         forward(s, cols).start()
+        issue_across(s + AHEAD)
         exchange_a(s)
+        pair = pick_row(merges, r, s)
+
+        @pl.when(pair > 0)
+        def _():
+            collect(pair - 1)
+
         forward(s, cols).wait_recv()
         late(hold, kind * crosses + k, cols)
 
@@ -360,11 +427,9 @@
             send_cross(k).start()
             send_cross_sums(k).start()
 
-        pair = pick_row(merges, r, s)
-
         @pl.when(pair > 0)
         def _():
-            merge(pair - 1)
+            pass_on(pair - 1)
 
     whole_a = sa_pair[...] + sa_in[0] + sa_in[1]
     total_tokens = tokens * groups
@@ -375,24 +440,28 @@
 
     @pl.loop(0, parts)
     def _(i):
-        s = steps - parts + i
+        s = main + i
         k = keeps + i
         cols = pl.ds(pl.multiple_of(t * band + i * LANES, LANES), LANES)
-        to_partner(s, cols).wait_recv()
+        partner_ready(s)
         early(k, cols)
-        to_across(s, cols).wait_recv()
-        forward(s, cols).start()
+        for h in (0, 1):
+            last_across(i, h, cols).wait_recv()
+            last_forward(s, h, cols).start()
+        part(k, across * rows, rows, cols)
         take_near(k)
         sb_half[2] = sb_near[k]
         for way, some in ((0, r > 0), (1, r < rings - 1)):
             @pl.when(some)
             def _():
-                j = (way * rings + r) * parts + i
+                j = way * (rings - 1) * parts + i
                 take_far(way, k, j)
                 sb_half[2] = sb_half[2] + sb_in[j]
 
-        forward(s, cols).wait_recv()
-        late(k, crosses + k, cols)
+        for h in (0, 1):
+            last_forward(s, h, cols).wait_recv()
+            part(k, (across + 1 - 2 * (across % 2)) * rows + h * (rows // 2), rows // 2, cols)
+        finish_sums(crosses + k)
         whole_b = sb_half[2] + sb_mine[crosses + k]
         mean_b = whole_b[0:1, :] * (1.0 / total_tokens)
         var_b = whole_b[1:2, :] * (1.0 / total_tokens) - mean_b * mean_b
@@ -418,9 +487,9 @@
     remote(b_hbm, own_b, px_send.at[0], px_recv.at[0], t, partner).wait_send()
     remote(own_b, own_b, fw_send.at[0], fw_recv.at[0], t, partner).wait_send()
     remote(cross_out, cross_in, c_send.at[0], c_recv.at[0], near, u).wait_send()
-    remote(sb_near, sb_near, cb_send.at[0], cb_recv.at[0], near, u).wait_send()
+    remote(sb_near, sb_near, cb_send.at[0], c_recv.at[0], near, u).wait_send()
     remote(far_out, far_out, f_send.at[0], f_recv.at[0], near, u).wait_send()
-    remote(sb_run, sb_run, fb_send.at[0], fb_recv.at[0], near, u).wait_send()
+    remote(sb_run, sb_run, fb_send.at[0], f_recv.at[0], near, u).wait_send()
 
 
 def fused(groups, plan, act_a, act_b):
@@ -447,20 +516,18 @@
             bf16(crosses, LANES, own),
             bf16(crosses, LANES, own),
             bf16(keeps, LANES, own),
-            bf16(2 * crosses, LANES, own),
+            bf16(2 * keeps, LANES, own),
             f32(8, own), f32(8, own), f32(8, own),
             f32(2, 8, own), f32(2, 8, own), f32(8, own),
             f32(3, 8, LANES),
             f32(2 * crosses, 8, LANES), f32(crosses, 8, LANES),
-            f32(keeps, 8, LANES), f32(2 * crosses, 8, LANES),
+            f32(keeps, 8, LANES), f32(2 * keeps, 8, LANES),
             pltpu.SemaphoreType.DMA, pltpu.SemaphoreType.DMA,
-            dma(1), dma(steps),
-            dma(1), dma(steps),
-            dma(1), dma(steps),
-            dma(1), dma(crosses),
-            dma(1), dma(crosses),
-            dma(1), dma(2 * crosses),
-            dma(1), dma(2 * crosses),
+            dma(1), dma(BUNCHES),
+            dma(1), dma(2 * AHEAD + 2 * parts),
+            dma(1), dma(4),
+            dma(1), dma(1), dma(crosses),
+            dma(1), dma(1), dma(2 * keeps),
             dma(1), dma(1),
             dma(2), dma(2),
         ],
@@ -479,7 +546,7 @@
         whole = act_a.shape[0] % 256 == 0 and act_a.shape[1] % LANES == 0
         if split == 4 and groups % 2 == 0 and groups > 4 and band % LANES == 0 and whole:
             plan = schedule(groups // 2, band // LANES)
-            if plan[-1]:
+            if plan[-1] and len(plan[0]) % BUNCHES == 0:
                 return fused(groups, plan, act_a, act_b)
         return plain(act_a, act_b)
 

time: 77.1 us -> 75.7 us (0.982)
  Pallas kernels: 75.9 us -> 74.6 us
    pallas_call x1, Pallas kernels: 75.9 us -> 74.6 us  [fused(): pl.pallas_call(functools.partial(kernel, groups, plan), out_shape=jax.Sha...]
where the time goes in v1:
time: 75.7 us; the launch traced here: 75.6 us
  Pallas kernels  74.6 us (99%)
  local copies, waits for them, and re-layouts  1.02 us (1%)
    pallas_call x1, Pallas kernels, fused(): pl.pallas_call(functools.partial(kernel, groups, plan), out_shape=jax.Sha...  74.6 us

profile of v1, /device:TPU:0, one launch (start us, length us, event | category | flops | bytes accessed | tf_op | source)
XLA Modules:
  0.0 75.6 jit_solution(1941092436235241094)
XLA Ops:
  0.0 74.6 %gather_correlate.1 = f32[384,768]{1,0:T(8,128)S(1)} custom-call(bf16[2048,768]{1,0:T(8,128)(2,1)} %a_hbm.1, bf16[512,3072]{1,0:T(8,128)(2,1)} %b_hbm.1), custom_call_target="tpu_custom_call" | custom-call | tf_op jit(solution)/shard_map/gather_correlate/pallas_call | solution.py:507
  74.6 1.0 %copy.4 = f32[384,768]{1,0:T(8,128)} copy(f32[384,768]{1,0:T(8,128)S(1)} %gather_correlate.1) | data formatting | bytes 2359296

commit v2 on v1

--- a/solution.py
+++ b/solution.py
@@ -113,7 +113,7 @@
 
 
 def encode(q):
-    size = jnp.exp2(jnp.minimum(jnp.abs(q), 1.04) * SPAN - BASE)
+    size = jnp.exp2(jnp.minimum(jnp.abs(q), 1.03) * SPAN - BASE)
     return jnp.where(q < 0, -size, size).astype(jnp.bfloat16)
 
 
@@ -127,7 +127,7 @@
            sa_own, sa_near, sa_pair, sa_in, sa_run, sa_stat, sb_half, sb_mine, sb_near, sb_run, sb_in,
            a_sem, b_sem, px_send, px_recv, nx_send, nx_recv, fw_send, fw_recv,
            c_send, cb_send, c_recv, f_send, fb_send, f_recv,
-           ca_send, ca_recv, fa_send, fa_recv):
+           ca_send, ca_recv, fa_send, fa_recv, ready, go):
     slots, orders, merges, _ = plan
     t = lax.axis_index("tok")
     u = lax.axis_index("unit")
@@ -175,7 +175,7 @@
         return remote(b_hbm.at[:, cols], block(g, u, cols), px_send.at[0], px_recv.at[s // bunch], t, partner)
 
     def to_across(s, cols):
-        return remote(b_hbm.at[:, cols], block(g, u, cols), nx_send.at[0], nx_recv.at[s % (2 * AHEAD)],
+        return remote(block(g, u, cols), block(g, u, cols), nx_send.at[0], nx_recv.at[s % (2 * AHEAD)],
                       t, across)
 
     def forward(s, cols):
@@ -187,7 +187,7 @@
         return g.at[pl.ds(pl.multiple_of(who * rows + h * size, size), size), cols]
 
     def last_across(i, h, cols):
-        return remote(b_hbm.at[pl.ds(h * (rows // 2), rows // 2), cols], piece(u, h, cols),
+        return remote(piece(u, h, cols), piece(u, h, cols),
                       nx_send.at[0], nx_recv.at[2 * AHEAD + 2 * i + h], t, across)
 
     def last_forward(s, h, cols):
@@ -230,39 +230,72 @@
 
     a_copy = pltpu.make_async_copy(a_hbm, a, a_sem)
     own_rows = pl.ds(pl.multiple_of(u * rows, rows), rows)
-    b_copy = pltpu.make_async_copy(b_hbm, g.at[own_rows, :], b_sem)
+
+    def b_copy(s):
+        cols = columns(*slot(s))
+        return pltpu.make_async_copy(
+            b_hbm.at[:, cols], g.at[own_rows, cols], b_sem.at[jnp.where(s == 0, 0, jnp.where(s < AHEAD, 1, 2))])
+
+    def b_wait(which, count):
+        cols = pl.ds(0, LANES * count)
+        pltpu.make_async_copy(b_hbm.at[:, cols], g.at[own_rows, cols], b_sem.at[which]).wait()
 
     barrier = pltpu.get_barrier_semaphore()
 
-    def greet(tt, uu):
-        pl.semaphore_signal(barrier, inc=1, device_id=(tt, uu), device_id_type=MESH)
-
-    greet(t, across)
-    greet(t, partner)
-    greet(near, u)
-
-    @pl.when(r > 0)
+    early_core = u % 2 == 0
+    wide_core = u % 2 == 1
+    peers = 1 + jnp.where(r > 0, 1, 0) + jnp.where(r < rings - 1, 1, 0)
+
+    def tell(sem, tt, uu):
+        pl.semaphore_signal(sem, inc=1, device_id=(tt, uu), device_id_type=MESH)
+
+    def tell_peers(sem):
+        tell(sem, near, u)
+
+        @pl.when(r > 0)
+        def _():
+            tell(sem, t - 2, u)
+
+        @pl.when(r < rings - 1)
+        def _():
+            tell(sem, t + 2, u)
+
+    tell(barrier, t, across)
+    tell(barrier, t, partner)
+
+    @pl.when(wide_core)
     def _():
-        greet(t - 2, u)
-
-    @pl.when(r < rings - 1)
+        tell_peers(barrier)
+
+    @pl.loop(0, AHEAD)
+    def _(s):
+        b_copy(s).start()
+
+    a_copy.start()
+    pl.semaphore_wait(barrier, 2 + jnp.where(wide_core, peers, 0))
+
+    @pl.when(wide_core)
     def _():
-        greet(t + 2, u)
-
-    a_copy.start()
-    b_copy.start()
-    pl.semaphore_wait(barrier, 3 + jnp.where(r > 0, 1, 0) + jnp.where(r < rings - 1, 1, 0))
+        tell_peers(ready)
+
+    b_wait(0, 1)
+    issue_across(jnp.int32(0))
+    b_wait(1, AHEAD - 1)
+
+    @pl.loop(1, AHEAD)
+    def _(s):
+        issue_across(s)
 
     @pl.loop(0, steps)
     def _(s):
-        @pl.when(s < AHEAD)
-        def _():
-            issue_across(s)
-
         to_partner(s, columns(*slot(s))).start()
 
+        @pl.when(s >= AHEAD)
+        def _():
+            b_copy(s).start()
+
+    b_wait(2, steps - AHEAD)
     a_copy.wait()
-    b_copy.wait()
     chunk = 128
 
     def sum_rows(wide):
@@ -278,6 +311,16 @@
     sa_own[...] = jnp.zeros((8, own), jnp.float32)
     sa_own[0:1, :] = jnp.sum(total, axis=0, keepdims=True)
     sa_own[1:2, :] = jnp.sum(square, axis=0, keepdims=True)
+
+    @pl.when(wide_core)
+    def _():
+        pl.semaphore_wait(ready, peers)
+        tell(go, t, partner)
+
+    @pl.when(early_core)
+    def _():
+        pl.semaphore_wait(go, 1)
+
     send_near_a.start()
 
     def tiles():
@@ -303,15 +346,6 @@
         sb_mine[k] = jnp.zeros((8, LANES), jnp.float32)
         sb_mine[k, 0:1, :] = jnp.sum(sb_half[0], axis=0, keepdims=True)
         sb_mine[k, 1:2, :] = jnp.sum(sb_half[1], axis=0, keepdims=True)
-
-    def late(hold, k, cols):
-        theirs = pl.ds(pl.multiple_of((1 - side) * half, half), half)
-        lhs = g[theirs, cols]
-        held[hold] = held[hold] + contract_tokens(lhs, a[theirs, :])
-        total, square = sum_rows(lhs)
-        sb_half[0] = sb_half[0] + total
-        sb_half[1] = sb_half[1] + square
-        finish_sums(k)
 
     def put(target, k, hold, sb, sa, share):
         tb, qb = sb[0:1, :], sb[1:2, :]
@@ -418,8 +452,10 @@
         def _():
             collect(pair - 1)
 
+        part(hold, across * rows, rows, cols)
         forward(s, cols).wait_recv()
-        late(hold, kind * crosses + k, cols)
+        part(hold, (across + 1 - 2 * (across % 2)) * rows, rows, cols)
+        finish_sums(kind * crosses + k)
 
         @pl.when(kind == 0)
         def _():
@@ -483,7 +519,7 @@
         send_run_a(1).wait_send()
 
     own_b = g.at[own_rows, :]
-    remote(b_hbm, own_b, nx_send.at[0], nx_recv.at[0], t, across).wait_send()
+    remote(own_b, own_b, nx_send.at[0], nx_recv.at[0], t, across).wait_send()
     remote(b_hbm, own_b, px_send.at[0], px_recv.at[0], t, partner).wait_send()
     remote(own_b, own_b, fw_send.at[0], fw_recv.at[0], t, partner).wait_send()
     remote(cross_out, cross_in, c_send.at[0], c_recv.at[0], near, u).wait_send()
@@ -522,7 +558,7 @@
             f32(3, 8, LANES),
             f32(2 * crosses, 8, LANES), f32(crosses, 8, LANES),
             f32(keeps, 8, LANES), f32(2 * keeps, 8, LANES),
-            pltpu.SemaphoreType.DMA, pltpu.SemaphoreType.DMA,
+            pltpu.SemaphoreType.DMA, dma(3),
             dma(1), dma(BUNCHES),
             dma(1), dma(2 * AHEAD + 2 * parts),
             dma(1), dma(4),
@@ -530,6 +566,7 @@
             dma(1), dma(1), dma(2 * keeps),
             dma(1), dma(1),
             dma(2), dma(2),
+            pltpu.SemaphoreType.REGULAR, pltpu.SemaphoreType.REGULAR,
         ],
         compiler_params=pltpu.CompilerParams(
             collective_id=0, has_side_effects=True, vmem_limit_bytes=52000 * 1024

time: 75.7 us -> 75.2 us (level)
  no operation moved by 1% of the time
where the time goes in v2:
time: 75.2 us; the launch traced here: 75 us
  Pallas kernels  74 us (98%)
  local copies, waits for them, and re-layouts  1.02 us (1%)
    pallas_call x1, Pallas kernels, fused(): pl.pallas_call(functools.partial(kernel, groups, plan), out_shape=jax.Sha...  74 us

profile of v2, /device:TPU:0, one launch (start us, length us, event | category | flops | bytes accessed | tf_op | source)
XLA Modules:
  0.0 75.0 jit_solution(7609798551106084986)
XLA Ops:
  0.0 74.0 %gather_correlate.1 = f32[384,768]{1,0:T(8,128)S(1)} custom-call(bf16[2048,768]{1,0:T(8,128)(2,1)} %a_hbm.1, bf16[512,3072]{1,0:T(8,128)(2,1)} %b_hbm.1), custom_call_target="tpu_custom_call" | custom-call | tf_op jit(solution)/shard_map/gather_correlate/pallas_call | solution.py:543
  74.0 1.0 %copy.4 = f32[384,768]{1,0:T(8,128)} copy(f32[384,768]{1,0:T(8,128)S(1)} %gather_correlate.1) | data formatting | bytes 2359296

commit v3 on v2

--- a/solution.py
+++ b/solution.py
@@ -9,8 +9,8 @@
 
 MESH = pl.DeviceIdType.MESH
 LANES = 128
-SPAN = 240.0
-BASE = 120.0
+SPAN = 244.0
+BASE = 122.0
 AHEAD = 4
 BUNCHES = 4
 
@@ -113,13 +113,15 @@
 
 
 def encode(q):
-    size = jnp.exp2(jnp.minimum(jnp.abs(q), 1.03) * SPAN - BASE)
+    size = jnp.clip(jnp.abs(q), 1e-30, 1.04)
+    size = jnp.exp2(size * lax.rsqrt(size) * SPAN - BASE)
     return jnp.where(q < 0, -size, size).astype(jnp.bfloat16)
 
 
 def decode(code):
     y = code.astype(jnp.float32)
     size = jnp.log2(jnp.abs(y)) + BASE
+    size = size * size
     return jnp.where(y < 0, -size, size)
 
 
@@ -360,7 +362,7 @@
     def take(hold, source, k, sb, sa, share):
         tb, qb = sb[0:1, :], sb[1:2, :]
         tb_col = column(tb * share)
-        norm_col = column(jnp.sqrt(spread(qb, tb, share)) * (1.0 / SPAN))
+        norm_col = column(jnp.sqrt(spread(qb, tb, share)) * (1.0 / (SPAN * SPAN)))
         for cols in tiles():
             ta = sa[0:1, cols]
             norm = jnp.sqrt(spread(sa[1:2, cols], ta, share))

time: 75.2 us -> 75.2 us (level)
  no operation moved by 1% of the time
where the time goes in v3:
time: 75.2 us; the launch traced here: 75 us
  Pallas kernels  74 us (98%)
  local copies, waits for them, and re-layouts  1.02 us (1%)
    pallas_call x1, Pallas kernels, fused(): pl.pallas_call(functools.partial(kernel, groups, plan), out_shape=jax.Sha...  74 us

profile of v3, /device:TPU:0, one launch (start us, length us, event | category | flops | bytes accessed | tf_op | source)
XLA Modules:
  0.0 75.0 jit_solution(9924347640536373562)
XLA Ops:
  0.0 74.0 %gather_correlate.1 = f32[384,768]{1,0:T(8,128)S(1)} custom-call(bf16[2048,768]{1,0:T(8,128)(2,1)} %a_hbm.1, bf16[512,3072]{1,0:T(8,128)(2,1)} %b_hbm.1), custom_call_target="tpu_custom_call" | custom-call | tf_op jit(solution)/shard_map/gather_correlate/pallas_call | solution.py:545
  74.0 1.0 %copy.4 = f32[384,768]{1,0:T(8,128)} copy(f32[384,768]{1,0:T(8,128)S(1)} %gather_correlate.1) | data formatting | bytes 2359296

commit v4 on v3

--- a/solution.py
+++ b/solution.py
@@ -125,7 +125,7 @@
     return jnp.where(y < 0, -size, size)
 
 
-def kernel(groups, plan, a_hbm, b_hbm, out, a, g, held, cross_out, cross_in, far_out, far_in,
+def work(groups, plan, a_hbm, b_hbm, out, a, g, held, cross_out, cross_in, far_out, far_in,
            sa_own, sa_near, sa_pair, sa_in, sa_run, sa_stat, sb_half, sb_mine, sb_near, sb_run, sb_in,
            a_sem, b_sem, px_send, px_recv, nx_send, nx_recv, fw_send, fw_recv,
            c_send, cb_send, c_recv, f_send, fb_send, f_recv,
@@ -483,12 +483,12 @@
         cols = pl.ds(pl.multiple_of(t * band + i * LANES, LANES), LANES)
         partner_ready(s)
         early(k, cols)
+        take_near(k)
+        sb_half[2] = sb_near[k]
         for h in (0, 1):
             last_across(i, h, cols).wait_recv()
             last_forward(s, h, cols).start()
-        part(k, across * rows, rows, cols)
-        take_near(k)
-        sb_half[2] = sb_near[k]
+            part(k, across * rows + h * (rows // 2), rows // 2, cols)
         for way, some in ((0, r > 0), (1, r < rings - 1)):
             @pl.when(some)
             def _():
@@ -530,6 +530,10 @@
     remote(sb_run, sb_run, fb_send.at[0], f_recv.at[0], near, u).wait_send()
 
 
+def kernel(groups, plan, semaphores, *refs):
+    pl.run_scoped(lambda *sems: work(groups, plan, *refs, *sems), *semaphores)
+
+
 def fused(groups, plan, act_a, act_b):
     tokens, own = act_a.shape
     rows, units = act_b.shape
@@ -542,8 +546,19 @@
     dma = lambda n: pltpu.SemaphoreType.DMA((n,))
     bf16 = lambda *shape: pltpu.VMEM(shape, jnp.bfloat16)
     f32 = lambda *shape: pltpu.VMEM(shape, jnp.float32)
+    semaphores = [
+        pltpu.SemaphoreType.DMA, dma(3),
+        dma(1), dma(BUNCHES),
+        dma(1), dma(2 * AHEAD + 2 * parts),
+        dma(1), dma(4),
+        dma(1), dma(1), dma(crosses),
+        dma(1), dma(1), dma(2 * keeps),
+        dma(1), dma(1),
+        dma(2), dma(2),
+        pltpu.SemaphoreType.REGULAR, pltpu.SemaphoreType.REGULAR,
+    ]
     return pl.pallas_call(
-        functools.partial(kernel, groups, plan),
+        functools.partial(kernel, groups, plan, semaphores),
         out_shape=jax.ShapeDtypeStruct((band, own), jnp.float32),
         in_specs=[pl.BlockSpec(memory_space=pltpu.HBM)] * 2,
         out_specs=pl.BlockSpec(memory_space=pltpu.VMEM),
@@ -560,15 +575,6 @@
             f32(3, 8, LANES),
             f32(2 * crosses, 8, LANES), f32(crosses, 8, LANES),
             f32(keeps, 8, LANES), f32(2 * keeps, 8, LANES),
-            pltpu.SemaphoreType.DMA, dma(3),
-            dma(1), dma(BUNCHES),
-            dma(1), dma(2 * AHEAD + 2 * parts),
-            dma(1), dma(4),
-            dma(1), dma(1), dma(crosses),
-            dma(1), dma(1), dma(2 * keeps),
-            dma(1), dma(1),
-            dma(2), dma(2),
-            pltpu.SemaphoreType.REGULAR, pltpu.SemaphoreType.REGULAR,
         ],
         compiler_params=pltpu.CompilerParams(
             collective_id=0, has_side_effects=True, vmem_limit_bytes=52000 * 1024

time: 75.2 us -> 74.6 us (level)
    pallas_call x1, Pallas kernels: 74 us -> 73.3 us  [fused(): pl.pallas_call(functools.partial(kernel, groups, plan, semaphores), out_s...]
where the time goes in v4:
time: 74.6 us; the launch traced here: 74.3 us
  Pallas kernels  73.3 us (98%)
  local copies, waits for them, and re-layouts  1.02 us (1%)
    pallas_call x1, Pallas kernels, fused(): pl.pallas_call(functools.partial(kernel, groups, plan, semaphores), out_s...  73.3 us

profile of v4, /device:TPU:0, one launch (start us, length us, event | category | flops | bytes accessed | tf_op | source)
XLA Modules:
  0.0 74.3 jit_solution(10970911305789673919)
XLA Ops:
  0.0 73.3 %gather_correlate.1 = f32[384,768]{1,0:T(8,128)S(1)} custom-call(bf16[2048,768]{1,0:T(8,128)(2,1)} %refs_0_.1, bf16[512,3072]{1,0:T(8,128)(2,1)} %refs_1_.1), custom_call_target="tpu_custom_call" | custom-call | tf_op jit(solution)/shard_map/gather_correlate/pallas_call | solution.py:560
  73.3 1.0 %copy.4 = f32[384,768]{1,0:T(8,128)} copy(f32[384,768]{1,0:T(8,128)S(1)} %gather_correlate.1) | data formatting | bytes 2359296

commit v5 on v4

--- a/solution.py
+++ b/solution.py
@@ -280,8 +280,9 @@
     def _():
         tell_peers(ready)
 
+    first = columns(*slot(jnp.int32(0)))
+    remote(b_hbm.at[:, first], block(g, u, first), nx_send.at[0], nx_recv.at[0], t, across).start()
     b_wait(0, 1)
-    issue_across(jnp.int32(0))
     b_wait(1, AHEAD - 1)
 
     @pl.loop(1, AHEAD)
@@ -589,6 +590,7 @@
     def per_device(act_a, act_b):
         band = act_b.shape[1] // groups
         whole = act_a.shape[0] % 256 == 0 and act_a.shape[1] % LANES == 0
+        whole = whole and act_a.shape[1] + 16 <= act_a.shape[0]
         if split == 4 and groups % 2 == 0 and groups > 4 and band % LANES == 0 and whole:
             plan = schedule(groups // 2, band // LANES)
             if plan[-1] and len(plan[0]) % BUNCHES == 0:

time: 74.6 us -> 74.2 us (level)
  no operation moved by 1% of the time
where the time goes in v5:
time: 74.2 us; the launch traced here: 74.1 us
  Pallas kernels  73 us (98%)
  local copies, waits for them, and re-layouts  1.02 us (1%)
    pallas_call x1, Pallas kernels, fused(): pl.pallas_call(functools.partial(kernel, groups, plan, semaphores), out_s...  73 us

profile of v5, /device:TPU:0, one launch (start us, length us, event | category | flops | bytes accessed | tf_op | source)
XLA Modules:
  0.0 74.1 jit_solution(17178280602319499723)
XLA Ops:
  0.0 73.0 %gather_correlate.1 = f32[384,768]{1,0:T(8,128)S(1)} custom-call(bf16[2048,768]{1,0:T(8,128)(2,1)} %refs_0_.1, bf16[512,3072]{1,0:T(8,128)(2,1)} %refs_1_.1), custom_call_target="tpu_custom_call" | custom-call | tf_op jit(solution)/shard_map/gather_correlate/pallas_call | solution.py:561
  73.0 1.0 %copy.4 = f32[384,768]{1,0:T(8,128)} copy(f32[384,768]{1,0:T(8,128)S(1)} %gather_correlate.1) | data formatting | bytes 2359296

commit v6 on v5

--- a/solution.py
+++ b/solution.py
@@ -337,13 +337,16 @@
         sb_half[0] = total
         sb_half[1] = square
 
-    def part(hold, start, size, cols):
+    def term(start, size, cols):
         some = pl.ds(pl.multiple_of(start, size), size)
         lhs = g[some, cols]
-        held[hold] = held[hold] + contract_tokens(lhs, a[some, :])
         total, square = sum_rows(lhs)
         sb_half[0] = sb_half[0] + total
         sb_half[1] = sb_half[1] + square
+        return contract_tokens(lhs, a[some, :])
+
+    def part(hold, start, size, cols):
+        held[hold] = held[hold] + term(start, size, cols)
 
     def finish_sums(k):
         sb_mine[k] = jnp.zeros((8, LANES), jnp.float32)
@@ -497,9 +500,11 @@
                 take_far(way, k, j)
                 sb_half[2] = sb_half[2] + sb_in[j]
 
-        for h in (0, 1):
-            last_forward(s, h, cols).wait_recv()
-            part(k, (across + 1 - 2 * (across % 2)) * rows + h * (rows // 2), rows // 2, cols)
+        theirs = (across + 1 - 2 * (across % 2)) * rows
+        last_forward(s, 0, cols).wait_recv()
+        part(k, theirs, rows // 2, cols)
+        last_forward(s, 1, cols).wait_recv()
+        rest = term(theirs + rows // 2, rows // 2, cols)
         finish_sums(crosses + k)
         whole_b = sb_half[2] + sb_mine[crosses + k]
         mean_b = whole_b[0:1, :] * (1.0 / total_tokens)
@@ -508,7 +513,7 @@
         inv_col = column(1.0 / jnp.sqrt(var_b + 1e-05))
         lanes = pl.ds(pl.multiple_of(i * LANES, LANES), LANES)
         for c in tiles():
-            centered = held[k, :, c] * (1.0 / total_tokens) - mean_col * sa_stat[0:1, c]
+            centered = (held[k, :, c] + rest[:, c]) * (1.0 / total_tokens) - mean_col * sa_stat[0:1, c]
             out[lanes, c] = centered * (inv_col * sa_stat[1:2, c])
 
     send_near_a.wait_send()

time: 74.2 us -> 74.2 us (level)
  no operation moved by 1% of the time
where the time goes in v6:
time: 74.2 us; the launch traced here: 74.1 us
  Pallas kernels  73.1 us (99%)
  local copies, waits for them, and re-layouts  1.02 us (1%)
    pallas_call x1, Pallas kernels, fused(): pl.pallas_call(functools.partial(kernel, groups, plan, semaphores), out_s...  73.1 us

profile of v6, /device:TPU:0, one launch (start us, length us, event | category | flops | bytes accessed | tf_op | source)
XLA Modules:
  0.0 74.1 jit_solution(8570367855007945602)
XLA Ops:
  0.0 73.1 %gather_correlate.1 = f32[384,768]{1,0:T(8,128)S(1)} custom-call(bf16[2048,768]{1,0:T(8,128)(2,1)} %refs_0_.1, bf16[512,3072]{1,0:T(8,128)(2,1)} %refs_1_.1), custom_call_target="tpu_custom_call" | custom-call | tf_op jit(solution)/shard_map/gather_correlate/pallas_call | solution.py:566
  73.1 1.0 %copy.4 = f32[384,768]{1,0:T(8,128)} copy(f32[384,768]{1,0:T(8,128)S(1)} %gather_correlate.1) | data formatting | bytes 2359296
